TPU v7x, 32 devices: a whole 2x2x4 slice. The times are simulated.
32 devices in a mesh: grp: 2 (over y), seq: 4 (over z), head: 2 (over x), batch: 2 (over core).
Axes of the slice: x: 2, y: 2, z: 4, core: 2. Of those that a mesh axis runs over, the one named last changes fastest.
Arguments:
- queries: bfloat16 [64, 64, 128], P(('grp', 'batch'), 'head'), parts along dimension 0, may hold values from -8 to 8
- key_cache: bfloat16 [64, 8, 1024, 128], P(('grp', 'batch'), 'head', 'seq'), parts along dimension 0, may hold values from -5 to 5
- value_cache: bfloat16 [64, 8, 1024, 128], P(('grp', 'batch'), 'head', 'seq'), parts along dimension 0, may hold values from -5 to 5
- gate_logits: float32 [2, 64, 64], P(None, ('grp', 'batch'), 'head'), parts along dimension 1, may hold values from -6 to 6
- lengths: int32 [64], P(('grp', 'batch')), parts along dimension 0, may hold values from 256 to 1024, as said below
- chosen: int32 [64, 8, 2], P(('grp', 'batch'), 'head'), parts along dimension 0, may hold values from 0 to 7, as said below
- counts: int32 [64, 8], P(('grp', 'batch'), 'head'), parts along dimension 0, may hold values from 1 to 2, as said below
Outputs:
- output: bfloat16 [64, 64, 128], P(('grp', 'batch'), 'head'), parts along dimension 0
There are 2 independent parts, one for each index of `grp`. A program takes and returns all parts, laid end to end along the dimension named above; each array names one. Nothing has to cross between parts.
Inputs may be any that keep to these rules, and one draw needn't show every extreme that they name: `lengths`: every draw has a sequence of the full length 1024. `chosen`: for each sequence and key-value head the first counts entries are distinct blocks that start below the sequence's length, and the first entry is block 0; the entries after them are ignored. `counts`: every draw has a sequence with 2 valid entries for every key-value head.
All inputs are finite; a program needn't handle non-finite values.
Results may differ from a plain program's by a relative error of at most 0.02.
Values may be sent and summed in bfloat16 or wider, within the bound.
A program may use at most 64 MiB of HBM per device.

v0:
```python
import functools
import math

import jax
import jax.numpy as jnp
from jax import lax
from jax.experimental import pallas as pl
from jax.experimental.pallas import tpu as pltpu
from jax.sharding import PartitionSpec as P

BLOCK = 128
LANES = 128
ROWS = 8
NEG = -1e30
MESH = pl.DeviceIdType.MESH


def kernel(
    n, q_ref, k_hbm, v_hbm, gate_ref, len_ref, chosen_ref, count_ref, o_ref,
    k_buf, v_buf, msg, stat, r_msg, r_stat,
    k_sem, v_sem, ms_sem, mr_sem, ss_sem, sr_sem, gs_sem, gr_sem,
):
    pairs, group, width = q_ref.shape
    tokens = k_hbm.shape[1]
    blocks = tokens // BLOCK
    own = pairs // n
    heads = count_ref.shape[0]
    slots = chosen_ref.shape[1]
    tiles = msg.shape[1] - own
    scale = 1.0 / math.sqrt(width)
    me = lax.axis_index("seq")

    holders = n // 2
    turns = n // holders
    low = (n - holders) // 2

    far = jnp.where(me < n // 2, (holders + 1) // 2, 0)

    def chunk_at(k):
        return lax.rem(lax.rem(k, holders) + far, holders) * turns + lax.div(k, holders)

    def owner(c):
        return low + lax.div(c, turns)

    def peer(r):
        return lax.rem(me + r, n)

    def load(k, hbm, buf, sem):
        return pltpu.make_async_copy(hbm.at[pl.ds(chunk_at(k) * own, own)], buf.at[k], sem.at[k])

    for k in range(n):
        load(k, k_hbm, k_buf, k_sem).start()
        load(k, v_hbm, v_buf, v_sem).start()

    barrier = pltpu.get_barrier_semaphore()
    holds = jnp.logical_and(me >= low, me < low + holders)
    for r in range(1, n):
        other = peer(r)

        @pl.when(jnp.logical_or(holds, jnp.logical_and(other >= low, other < low + holders)))
        def _(other=other):
            pl.semaphore_signal(barrier, inc=1, device_id={"seq": other}, device_id_type=MESH)

    lane = lax.broadcasted_iota(jnp.int32, (ROWS, LANES), 1)
    row = lax.broadcasted_iota(jnp.int32, (ROWS, LANES), 0)

    lane_pair = lax.div(lane, group)

    def gate_row(branch, first_pair):
        if own % heads == 0:
            first = lax.div(first_pair, heads)
            pieces = [gate_ref[branch, pl.ds(first + r, 1), :] for r in range(own // heads)]
        else:
            first = first_pair
            line = gate_ref[branch, pl.ds(lax.div(first, heads), 1), :]
            picked = line[:, : own * group]
            for o in range(1, heads // own):
                here = lax.rem(first, heads) == o * own
                picked = jnp.where(here, line[:, o * own * group : (o + 1) * own * group], picked)
            pieces = [picked]
        if own * group < LANES:
            pieces.append(jnp.zeros((1, LANES - own * group), jnp.float32))
        return jax.nn.sigmoid(jnp.concatenate(pieces, axis=1))

    all_gates = []
    for turn in range(turns):
        gate_pair = lax.rem((me - low) * turns + turn + n, n) * own
        all_gates.append(jnp.where(row == 0, gate_row(1, gate_pair), gate_row(0, gate_pair)))
    token = lax.broadcasted_iota(jnp.int32, (BLOCK, LANES), 0)

    def send(k, held, landed, send_sem, recv_sem):
        c = chunk_at(k)
        turn = lax.rem(c, turns)
        slot = lax.rem(me - owner(c) + n, n) - 1
        return pltpu.make_async_remote_copy(
            src_ref=held.at[k], dst_ref=landed.at[turn, slot],
            send_sem=send_sem.at[k], recv_sem=recv_sem.at[turn, slot],
            device_id={"seq": owner(c)}, device_id_type=MESH,
        )

    def arrival(turn, slot, held, landed, send_sem, recv_sem):
        return pltpu.make_async_remote_copy(
            src_ref=held.at[0], dst_ref=landed.at[turn, slot],
            send_sem=send_sem.at[0], recv_sem=recv_sem.at[turn, slot],
            device_id={"seq": peer(1 + slot)}, device_id_type=MESH,
        )

    stat_path = (stat, r_stat, ss_sem, sr_sem)
    msg_path = (msg, r_msg, ms_sem, mr_sem)

    def part(k, carry):
        target = chunk_at(k)
        first = target * own
        lengths = [len_ref[lax.div(first + i, heads)] for i in range(own)]

        def spread(values):
            line = jnp.full((1, LANES), values[0], jnp.int32)
            for i in range(1, own):
                line = jnp.where(lane_pair[:1] == i, values[i], line)
            return line

        length_line = spread(lengths)
        pair_ids = [(lax.rem(first + i, heads), lax.div(first + i, heads)) for i in range(own)]
        count_line = spread([count_ref[h, b] for h, b in pair_ids])
        chosen_lines = [spread([chosen_ref[h, slot, b] for h, b in pair_ids]) for slot in range(slots)]
        chosen_lines = [jnp.where(slot < count_line, line, -1) for slot, line in enumerate(chosen_lines)]

        rows = q_ref[pl.ds(first, own)].astype(jnp.float32).reshape(own * group, width)
        if own * group < LANES:
            rows = jnp.concatenate([rows, jnp.zeros((LANES - own * group, width), jnp.float32)], axis=0)
        columns = rows.T
        load(k, k_hbm, k_buf, k_sem).wait()
        scores = None
        for i in range(0, own, 2):
            both = range(i, min(i + 2, own))
            held = jnp.concatenate(
                [jnp.where(lane_pair[:1] == p, columns, 0.0) for p in both], axis=0
            ).astype(jnp.bfloat16)
            keys = jnp.concatenate([k_buf[k, p] for p in both], axis=1)
            product = jnp.dot(keys, held, preferred_element_type=jnp.float32)
            scores = product if scores is None else scores + product
        scores = scores * scale

        stats = jnp.zeros((ROWS, LANES), jnp.float32)
        masked, inside = [], []
        for j in range(blocks):
            block = me * blocks + j
            filled = jnp.clip(length_line - block * BLOCK, 0, BLOCK)
            hits = [line == block for line in chosen_lines]
            limit = jnp.where(functools.reduce(jnp.logical_or, hits), filled, 0)
            block_scores = scores[j * BLOCK : (j + 1) * BLOCK]
            root = lax.rsqrt(jnp.maximum(filled, 1).astype(jnp.float32))
            total = jnp.sum(jnp.where(token < filled, block_scores, 0.0), axis=0, keepdims=True)
            stats = jnp.where(row == 1 + j, jnp.where(filled > 0, total * root, NEG), stats)
            inside.append(token < limit)
            masked.append(jnp.where(inside[j], block_scores, NEG))
        top = jnp.max(functools.reduce(jnp.maximum, masked), axis=0, keepdims=True)
        weights = [jnp.where(i, jnp.exp(m - top), 0.0) for i, m in zip(inside, masked)]
        weight_sum = jnp.sum(functools.reduce(jnp.add, weights), axis=0, keepdims=True)
        safe_sum = jnp.maximum(weight_sum, 1.0)
        log_sum = jnp.where(weight_sum > 0.0, top + jnp.log(safe_sum), NEG)
        stats = jnp.where(row == 0, log_sum, stats)
        stat[k] = stats
        inverse = 1.0 / safe_sum
        weight_rows = jnp.concatenate([(w * inverse).T for w in weights], axis=1)

        load(k, v_hbm, v_buf, v_sem).wait()
        per_tile = ROWS // blocks
        for tile in range(tiles):
            members = range(tile * per_tile, min((tile + 1) * per_tile, own))
            length_rows = jnp.zeros((ROWS, LANES), jnp.int32)
            for at, i in enumerate(members):
                length_rows = jnp.where(lax.div(row, blocks) == at, lengths[i], length_rows)
            start_rows = (me * blocks + lax.rem(row, blocks)) * BLOCK
            filled_rows = jnp.clip(length_rows - start_rows, 0, BLOCK)
            root_rows = lax.rsqrt(jnp.maximum(filled_rows, 1).astype(jnp.float32))
            live = lane < filled_rows
            pooled = jnp.zeros((ROWS, width), jnp.float32)
            for at, i in enumerate(members):
                live_rows = jnp.concatenate(
                    [jnp.where(live & (row == at * blocks + j), 1.0, 0.0) for j in range(blocks)], axis=1
                )
                left = jnp.concatenate([weight_rows[i * group : (i + 1) * group], live_rows], axis=0)
                summed = jnp.dot(
                    left.astype(jnp.bfloat16), v_buf[k, i], preferred_element_type=jnp.float32
                )
                msg[k, i] = summed[:group].astype(jnp.bfloat16)
                pooled = pooled + summed[group:]
            msg[k, own + tile] = (pooled * root_rows).astype(jnp.bfloat16)

        @pl.when(k == 0)
        def _():
            pl.semaphore_wait(barrier, jnp.where(holds, n - 1, holders))

        @pl.when(owner(target) != me)
        def _():
            send(k, *stat_path).start()
            send(k, *msg_path).start()

        return carry

    lax.fori_loop(0, n, part, 0, unroll=4)

    def share(turn, r):
        c = (me - low) * turns + turn
        rows = o_ref.at[pl.ds(c * own, own)]
        return pltpu.make_async_remote_copy(
            src_ref=rows, dst_ref=rows, send_sem=gs_sem.at[turn, r - 1], recv_sem=gr_sem.at[c],
            device_id={"seq": peer(r)}, device_id_type=MESH,
        )

    def finish(turn):
        c = (me - low) * turns + turn
        home = turn * holders + lax.rem(me - low + holders - far, holders)
        gates = all_gates[turn]
        for slot in range(n - 1):
            arrival(turn, slot, *stat_path).wait_recv()
        all_stats = [r_stat[turn, slot] for slot in range(n - 1)] + [stat[home]]
        top = functools.reduce(jnp.maximum, all_stats)
        block_row = (row >= 1) & (row <= blocks)
        block_top = jnp.max(jnp.where(block_row, top, NEG), axis=0, keepdims=True)
        top = jnp.where(row == 0, top, block_top)
        shares = [jnp.where(row <= blocks, jnp.exp(s - top), 0.0) for s in all_stats]
        total = functools.reduce(jnp.add, shares)
        block_total = jnp.sum(jnp.where(block_row, total, 0.0), axis=0, keepdims=True)
        factor = gates / jnp.where(row == 0, total, block_total)
        shares = [s * factor for s in shares]
        per_turn = LANES // ROWS
        turned = []
        for k in range(0, n, per_turn):
            stack = shares[k : k + per_turn]
            if len(stack) < per_turn:
                stack.append(jnp.zeros((LANES - len(stack) * ROWS, LANES), jnp.float32))
            turned.append(jnp.concatenate(stack, axis=0).T)

        def coefficient(k, i, which):
            at = (k % per_turn) * ROWS + which
            return turned[k // per_turn][i * group : (i + 1) * group, at : at + 1]

        for slot in range(n - 1):
            arrival(turn, slot, *msg_path).wait_recv()
        for tile in range(tiles):
            tile_rows = [r_msg[turn, slot, own + tile].astype(jnp.float32) for slot in range(n - 1)]
            tile_rows.append(msg[home, own + tile].astype(jnp.float32))
            for i in range(own):
                if (i * blocks) // ROWS != tile:
                    continue
                base = (i * blocks) % ROWS
                total = jnp.zeros((ROWS, width), jnp.float32)
                for k in range(n):
                    partial = msg[home, i] if k == n - 1 else r_msg[turn, k, i]
                    total += coefficient(k, i, 0) * partial.astype(jnp.float32)
                    for j in range(blocks):
                        total += coefficient(k, i, 1 + j) * tile_rows[k][base + j : base + j + 1, :]
                o_ref[c * own + i] = total.astype(jnp.bfloat16)
        for r in range(1, n):
            share(turn, r).start()

    @pl.when(holds)
    def _():
        for turn in range(turns):
            finish(turn)

    def drain(k, carry):
        @pl.when(owner(chunk_at(k)) != me)
        def _():
            send(k, *stat_path).wait_send()
            send(k, *msg_path).wait_send()

        return carry

    def collect(c, carry):
        @pl.when(owner(c) != me)
        def _():
            rows = o_ref.at[pl.ds(c * own, own)]
            pltpu.make_async_remote_copy(
                src_ref=rows, dst_ref=rows, send_sem=gs_sem.at[0, 0], recv_sem=gr_sem.at[c],
                device_id={"seq": owner(c)}, device_id_type=MESH,
            ).wait_recv()

        return carry

    lax.fori_loop(0, n, drain, 0)
    lax.fori_loop(0, n, collect, 0)

    @pl.when(holds)
    def _():
        for turn in range(turns):
            for r in range(1, n):
                share(turn, r).wait_send()


def on_device(n, queries, key_cache, value_cache, gate_logits, lengths, chosen, counts):
    batch_rows, head_count, context, width = key_cache.shape
    pairs = batch_rows * head_count
    group = queries.shape[1] // head_count
    blocks = context // BLOCK
    own = pairs // n
    tiles = -(-own * blocks // ROWS)
    assert n % 2 == 0 and pairs % n == 0 and group == ROWS and ROWS % blocks == 0
    assert own * group <= LANES and 1 + blocks <= ROWS and width == LANES
    vmem = pl.BlockSpec(memory_space=pltpu.VMEM)
    smem = pl.BlockSpec(memory_space=pltpu.SMEM)
    hbm = pl.BlockSpec(memory_space=pl.ANY)
    turns = n // (n // 2)
    dma = pltpu.SemaphoreType.DMA((n,))
    dma2 = pltpu.SemaphoreType.DMA((turns, n - 1))
    output = pl.pallas_call(
        functools.partial(kernel, n),
        out_shape=pltpu.VMEM((pairs, group, width), jnp.bfloat16),
        in_specs=[vmem, hbm, hbm, vmem, smem, smem, smem],
        out_specs=vmem,
        scratch_shapes=[
            pltpu.VMEM((n, own, context, width), jnp.bfloat16),
            pltpu.VMEM((n, own, context, width), jnp.bfloat16),
            pltpu.VMEM((n, own + tiles, group, width), jnp.bfloat16),
            pltpu.VMEM((n, ROWS, LANES), jnp.float32),
            pltpu.VMEM((turns, n - 1, own + tiles, group, width), jnp.bfloat16),
            pltpu.VMEM((turns, n - 1, ROWS, LANES), jnp.float32),
            dma, dma, dma, dma2, dma, dma2, dma2, dma,
        ],
        compiler_params=pltpu.CompilerParams(collective_id=0, has_side_effects=True),
    )(
        queries.reshape(pairs, group, width),
        key_cache.reshape(pairs, context, width),
        value_cache.reshape(pairs, context, width),
        gate_logits,
        lengths,
        chosen.transpose(1, 2, 0),
        counts.transpose(1, 0),
    )
    return output.reshape(batch_rows, head_count * group, width)


def solution(mesh):
    return jax.shard_map(
        functools.partial(on_device, mesh.shape["seq"]),
        mesh=mesh,
        in_specs=(
            P(("grp", "batch"), "head", None),
            P(("grp", "batch"), "head", "seq", None),
            P(("grp", "batch"), "head", "seq", None),
            P(None, ("grp", "batch"), "head"),
            P(("grp", "batch")),
            P(("grp", "batch"), "head", None),
            P(("grp", "batch"), "head"),
        ),
        out_specs=P(("grp", "batch"), "head", None),
        check_vma=False,
    )
```

profile of v0, /device:TPU:0, one launch (start us, length us, event | category | flops | bytes accessed | tf_op | source)
XLA Modules:
  0.0 17.0 jit_solution(4077933057805888400)
XLA Ops:
  0.0 16.3 %shard_map.73 = bf16[64,8,128]{2,1,0:T(8,128)(2,1)S(1)} custom-call(bf16[64,8,128]{2,1,0:T(8,128)(2,1)} %bitcast.9, bf16[64,256,128]{2,1,0:T(8,128)(2,1)} %bitcast.7, bf16[64,256,128]{2,1,0:T(8,128)(2,1)} %bitcast.8, f32[2,16,32]{2,1,0:T(8,128)} %gate_ref.1, s32[16]{0:T(128)} %len_ref.1, s32[4,2,16]{2,1,0:T(2,128)} %bitcast.10, s32[4,16]{1,0:T(4,128)} %bitcast.11), custom_call_target="tpu_custom_call" | custom-call | tf_op jit(solution)/shard_map/pallas_call | solution.py:308
  16.3 0.7 %copy.9 = bf16[16,32,128]{2,1,0:T(8,128)(2,1)} copy(bf16[16,32,128]{2,1,0:T(8,128)(2,1)S(1)} %bitcast.6) | data formatting | bytes 262144
where the time goes:
time: 17.2 us; the launch traced here: 17 us
  Pallas kernels  16.3 us (95%)
  local copies, waits for them, and re-layouts  0.66 us (4%)
    pallas_call x1, Pallas kernels, on_device(): pl.pallas_call(functools.partial(kernel, n), out_shape=pltpu.VMEM((pairs,...  16.3 us
    unnamed x1, local copies, waits for them, and re-layouts  0.66 us

commit v1 on v0

v1 whole, which is shorter than its diff:
```python
import functools
import math

import jax
import jax.numpy as jnp
from jax import lax
from jax.experimental import pallas as pl
from jax.experimental.pallas import tpu as pltpu
from jax.sharding import PartitionSpec as P

BLOCK = 128
LANES = 128
ROWS = 8
NEG = -1e30
MESH = pl.DeviceIdType.MESH


def owners_of(n, chunks):
    if chunks >= 2 * n and n >= 3:
        return [0, 0] + [2 - c % 2 for c in range(chunks - 3)] + [0]
    return [c * n // chunks for c in range(chunks)]


def plan_of(n, pairs, group):
    size = min(pairs, LANES // group)
    parts = pairs // size
    cuts = max(2, n // parts)
    return size, parts, cuts


def kernel(
    n, q_ref, k_hbm, v_hbm, gate_ref, len_ref, chosen_ref, count_ref, o_ref,
    k_buf, v_buf, msg, r_msg, gates,
    k_sem, v_sem, ms_sem, mr_sem, gs_sem, gr_sem,
):
    pairs, tokens, width = k_hbm.shape
    group = q_ref.shape[0] // pairs
    blocks = tokens // BLOCK
    heads = count_ref.shape[0]
    slots = chosen_ref.shape[1]
    size, parts, cuts = plan_of(n, pairs, group)
    own = size // cuts
    chunks = parts * cuts
    owners = owners_of(n, chunks)
    holders = sorted(set(owners))
    owned = {o: [c for c in range(chunks) if owners[c] == o] for o in holders}
    most = max(len(v) for v in owned.values())
    span = own * group
    pooled_rows = -(-own * blocks // ROWS) * ROWS
    stat_at = span + pooled_rows
    per_tile = ROWS // blocks
    scale = 1.0 / math.sqrt(width)
    me = lax.axis_index("seq")

    def load(k, hbm, buf, sem):
        return pltpu.make_async_copy(hbm.at[pl.ds(k * size, size)], buf.at[k], sem.at[k])

    for k in range(parts):
        load(k, k_hbm, k_buf, k_sem).start()
        load(k, v_hbm, v_buf, v_sem).start()

    barrier = pltpu.get_barrier_semaphore()
    holds = functools.reduce(jnp.logical_or, [me == o for o in holders])

    @pl.when(holds)
    def _():
        for r in range(1, n):
            pl.semaphore_signal(
                barrier, inc=1, device_id={"seq": lax.rem(me + r, n)}, device_id_type=MESH
            )

    lane = lax.broadcasted_iota(jnp.int32, (ROWS, LANES), 1)
    row = lax.broadcasted_iota(jnp.int32, (ROWS, LANES), 0)
    lane_pair = lax.div(lane, group)
    token = lax.broadcasted_iota(jnp.int32, (BLOCK, LANES), 0)

    def gate_row(branch, first):
        pieces = []
        at = first
        while at < first + own:
            b, h = divmod(at, heads)
            run = min(heads - h, first + own - at)
            pieces.append(gate_ref[branch, b : b + 1, h * group : (h + run) * group])
            at += run
        if span < LANES:
            pieces.append(jnp.zeros((1, LANES - span), jnp.float32))
        return jax.nn.sigmoid(jnp.concatenate(pieces, axis=1))

    for c in range(chunks):
        gates[c] = jnp.where(row == 0, gate_row(1, c * own), gate_row(0, c * own))

    def send(c):
        slot = lax.rem(me - owners[c] + n, n) - 1
        at = owned[owners[c]].index(c)
        return pltpu.make_async_remote_copy(
            src_ref=msg.at[c], dst_ref=r_msg.at[at, slot],
            send_sem=ms_sem.at[c], recv_sem=mr_sem.at[at, slot],
            device_id={"seq": owners[c]}, device_id_type=MESH,
        )

    def arrival(at, slot):
        return pltpu.make_async_remote_copy(
            src_ref=msg.at[0], dst_ref=r_msg.at[at, slot],
            send_sem=ms_sem.at[0], recv_sem=mr_sem.at[at, slot],
            device_id={"seq": lax.rem(me + 1 + slot, n)}, device_id_type=MESH,
        )

    def spread(values):
        line = jnp.full((1, LANES), values[0], jnp.int32)
        for i in range(1, size):
            line = jnp.where(lane_pair[:1] == i, values[i], line)
        return line

    def part(k):
        first = k * size
        ids = [divmod(first + i, heads) for i in range(size)]
        lengths = [len_ref[b] for b, _ in ids]
        length_line = spread(lengths)
        count_line = spread([count_ref[h, b] for b, h in ids])
        chosen_lines = [spread([chosen_ref[h, slot, b] for b, h in ids]) for slot in range(slots)]
        chosen_lines = [jnp.where(slot < count_line, line, -1) for slot, line in enumerate(chosen_lines)]

        rows = q_ref[first * group : (first + size) * group, :].astype(jnp.float32)
        if size * group < LANES:
            rows = jnp.concatenate([rows, jnp.zeros((LANES - size * group, width), jnp.float32)], axis=0)
        columns = rows.T
        load(k, k_hbm, k_buf, k_sem).wait()
        scores = None
        for i in range(0, size, 2):
            both = range(i, min(i + 2, size))
            held = jnp.concatenate(
                [jnp.where(lane_pair[:1] == p, columns, 0.0) for p in both], axis=0
            ).astype(jnp.bfloat16)
            keys = jnp.concatenate([k_buf[k, p] for p in both], axis=1)
            product = jnp.dot(keys, held, preferred_element_type=jnp.float32)
            scores = product if scores is None else scores + product
        scores = scores * scale

        stats = jnp.full((ROWS, LANES), NEG, jnp.float32)
        masked, inside = [], []
        for j in range(blocks):
            block = me * blocks + j
            filled = jnp.clip(length_line - block * BLOCK, 0, BLOCK)
            hits = [line == block for line in chosen_lines]
            limit = jnp.where(functools.reduce(jnp.logical_or, hits), filled, 0)
            block_scores = scores[j * BLOCK : (j + 1) * BLOCK]
            root = lax.rsqrt(jnp.maximum(filled, 1).astype(jnp.float32))
            total = jnp.sum(jnp.where(token < filled, block_scores, 0.0), axis=0, keepdims=True)
            stats = jnp.where(row == 1 + j, jnp.where(filled > 0, total * root, NEG), stats)
            inside.append(token < limit)
            masked.append(jnp.where(inside[j], block_scores, NEG))
        top = jnp.max(functools.reduce(jnp.maximum, masked), axis=0, keepdims=True)
        weights = [jnp.where(i, jnp.exp(m - top), 0.0) for i, m in zip(inside, masked)]
        weight_sum = jnp.sum(functools.reduce(jnp.add, weights), axis=0, keepdims=True)
        safe_sum = jnp.maximum(weight_sum, 1.0)
        log_sum = jnp.where(weight_sum > 0.0, top + jnp.log(safe_sum), NEG)
        stats = jnp.where(row == 0, log_sum, stats)
        high = stats.astype(jnp.bfloat16).astype(jnp.float32)
        low = stats - high
        half = ROWS // 2
        parted = jnp.concatenate([high[:half], low[:half]], axis=0)
        inverse = 1.0 / safe_sum
        weight_rows = jnp.concatenate([(w * inverse).T for w in weights], axis=1)

        load(k, v_hbm, v_buf, v_sem).wait()
        for cut in range(cuts):
            c = k * cuts + cut
            outs, tiles = [], []
            for i in range(cut * own, (cut + 1) * own):
                at = (i - cut * own) % per_tile
                if at == 0:
                    members = range(i, min(i + per_tile, (cut + 1) * own))
                    length_rows = jnp.zeros((ROWS, LANES), jnp.int32)
                    for m, p in enumerate(members):
                        length_rows = jnp.where(lax.div(row, blocks) == m, lengths[p], length_rows)
                    start_rows = (me * blocks + lax.rem(row, blocks)) * BLOCK
                    filled_rows = jnp.clip(length_rows - start_rows, 0, BLOCK)
                    root_rows = lax.rsqrt(jnp.maximum(filled_rows, 1).astype(jnp.float32))
                    live = lane < filled_rows
                    pooled = jnp.zeros((ROWS, width), jnp.float32)
                live_rows = jnp.concatenate(
                    [jnp.where(live & (row == at * blocks + j), 1.0, 0.0) for j in range(blocks)], axis=1
                )
                left = jnp.concatenate([weight_rows[i * group : (i + 1) * group], live_rows], axis=0)
                summed = jnp.dot(left.astype(jnp.bfloat16), v_buf[k, i], preferred_element_type=jnp.float32)
                outs.append(summed[:group])
                pooled = pooled + summed[group:]
                if at == per_tile - 1 or i == (cut + 1) * own - 1:
                    tiles.append(pooled * root_rows)
            turned = parted
            if cut:
                turned = pltpu.roll(parted, LANES - cut * span, 1)
            msg[c] = jnp.concatenate(outs + tiles + [turned], axis=0).astype(jnp.bfloat16)

        if k == 0:
            pl.semaphore_wait(barrier, jnp.where(holds, len(holders) - 1, len(holders)))

        for cut in range(cuts):
            c = k * cuts + cut

            @pl.when(me != owners[c])
            def _(c=c):
                send(c).start()

    for k in range(parts):
        part(k)

    def pick(at):
        c = 0
        for o in holders:
            if at < len(owned[o]):
                c = jnp.where(me == o, owned[o][at], c)
        return c

    def has(at):
        return functools.reduce(jnp.logical_or, [me == o for o in holders if at < len(owned[o])])

    def spot(c):
        return pl.ds(pl.multiple_of(c * span, span), span)

    def share(at, r):
        rows = o_ref.at[spot(pick(at))]
        return pltpu.make_async_remote_copy(
            src_ref=rows, dst_ref=rows, send_sem=gs_sem.at[at, r - 1], recv_sem=gr_sem.at[pick(at)],
            device_id={"seq": lax.rem(me + r, n)}, device_id_type=MESH,
        )

    def finish(at):
        c = pick(at)
        for slot in range(n - 1):
            arrival(at, slot).wait_recv()
        half = ROWS // 2
        halves = row[:half]
        parts_in = [r_msg.at[at, slot] for slot in range(n - 1)] + [msg.at[c]]
        all_stats = []
        for ref in parts_in:
            parted = ref[stat_at : stat_at + ROWS, :].astype(jnp.float32)
            all_stats.append(parted[:half] + parted[half:])
        top = functools.reduce(jnp.maximum, all_stats)
        block_row = (halves >= 1) & (halves <= blocks)
        block_top = jnp.max(jnp.where(block_row, top, NEG), axis=0, keepdims=True)
        top = jnp.where(halves == 0, top, block_top)
        shares = [jnp.where(halves <= blocks, jnp.exp(s - top), 0.0) for s in all_stats]
        total = functools.reduce(jnp.add, shares)
        block_total = jnp.sum(jnp.where(block_row, total, 0.0), axis=0, keepdims=True)
        factor = gates[c][:half] / jnp.where(halves == 0, total, block_total)
        wide = lax.broadcasted_iota(jnp.int32, (span, LANES), 1)
        tall = lax.broadcasted_iota(jnp.int32, (span, LANES), 0)
        pool_lane = lax.broadcasted_iota(jnp.int32, (pooled_rows, LANES), 1)
        pool_row = lax.broadcasted_iota(jnp.int32, (pooled_rows, LANES), 0)
        mine = lax.div(pool_lane, group) == lax.div(pool_row, blocks)
        out = None
        for ref, s in zip(parts_in, shares):
            factors = s * factor
            pick_rows = jnp.where(wide == tall, factors[:1], 0.0)
            level = jnp.broadcast_to(factors[1:2], (pooled_rows, LANES))
            for j in range(1, blocks):
                level = jnp.where(lax.rem(pool_row, blocks) == j, factors[1 + j : 2 + j], level)
            level = jnp.where(mine, level, 0.0)
            left = jnp.concatenate([pick_rows, level], axis=0).astype(jnp.bfloat16)[:, :span]
            term = lax.dot_general(
                left, ref[:stat_at, :], (((0,), (0,)), ((), ())), preferred_element_type=jnp.float32
            )
            out = term if out is None else out + term
        o_ref[spot(c), :] = out.astype(jnp.bfloat16)
        for r in range(n - 1, 0, -1):
            share(at, r).start()

    for at in range(most):

        @pl.when(has(at))
        def _(at=at):
            finish(at)

    for c in range(chunks):

        @pl.when(me != owners[c])
        def _(c=c):
            send(c).wait_send()

    for c in range(chunks):

        @pl.when(me != owners[c])
        def _(c=c):
            rows = o_ref.at[c * span : (c + 1) * span]
            pltpu.make_async_remote_copy(
                src_ref=rows, dst_ref=rows, send_sem=gs_sem.at[0, 0], recv_sem=gr_sem.at[c],
                device_id={"seq": owners[c]}, device_id_type=MESH,
            ).wait_recv()

    for at in range(most):

        @pl.when(has(at))
        def _(at=at):
            for r in range(1, n):
                share(at, r).wait_send()


def on_device(n, queries, key_cache, value_cache, gate_logits, lengths, chosen, counts):
    batch_rows, head_count, context, width = key_cache.shape
    pairs = batch_rows * head_count
    group = queries.shape[1] // head_count
    blocks = context // BLOCK
    size, parts, cuts = plan_of(n, pairs, group)
    own = size // cuts
    chunks = parts * cuts
    owners = owners_of(n, chunks)
    most = max(owners.count(o) for o in owners)
    assert group == ROWS and ROWS % blocks == 0 and width == LANES
    assert 1 + blocks <= ROWS // 2 and size % cuts == 0 and pairs % size == 0
    rows = own * group + -(-own * blocks // ROWS) * ROWS + ROWS
    vmem = pl.BlockSpec(memory_space=pltpu.VMEM)
    smem = pl.BlockSpec(memory_space=pltpu.SMEM)
    hbm = pl.BlockSpec(memory_space=pl.ANY)
    dma = pltpu.SemaphoreType.DMA
    output = pl.pallas_call(
        functools.partial(kernel, n),
        out_shape=pltpu.VMEM((pairs * group, width), jnp.bfloat16),
        in_specs=[vmem, hbm, hbm, vmem, smem, smem, smem],
        out_specs=vmem,
        scratch_shapes=[
            pltpu.VMEM((parts, size, context, width), jnp.bfloat16),
            pltpu.VMEM((parts, size, context, width), jnp.bfloat16),
            pltpu.VMEM((chunks, rows, width), jnp.bfloat16),
            pltpu.VMEM((most, n - 1, rows, width), jnp.bfloat16),
            pltpu.VMEM((chunks, ROWS, LANES), jnp.float32),
            dma((parts,)), dma((parts,)), dma((chunks,)), dma((most, n - 1)), dma((most, n - 1)), dma((chunks,)),
        ],
        compiler_params=pltpu.CompilerParams(collective_id=0, has_side_effects=True),
    )(
        queries.reshape(pairs * group, width),
        key_cache.reshape(pairs, context, width),
        value_cache.reshape(pairs, context, width),
        gate_logits,
        lengths,
        chosen.transpose(1, 2, 0),
        counts.transpose(1, 0),
    )
    return output.reshape(batch_rows, head_count * group, width)


def solution(mesh):
    return jax.shard_map(
        functools.partial(on_device, mesh.shape["seq"]),
        mesh=mesh,
        in_specs=(
            P(("grp", "batch"), "head", None),
            P(("grp", "batch"), "head", "seq", None),
            P(("grp", "batch"), "head", "seq", None),
            P(None, ("grp", "batch"), "head"),
            P(("grp", "batch")),
            P(("grp", "batch"), "head", None),
            P(("grp", "batch"), "head"),
        ),
        out_specs=P(("grp", "batch"), "head", None),
        check_vma=False,
    )
```

time: 17.2 us -> 16.6 us (0.965)
  Pallas kernels: 16.3 us -> 15.8 us
    pallas_call x1, Pallas kernels: 16.3 us -> 15.8 us  [on_device(): pl.pallas_call(functools.partial(kernel, n), out_shape=pltpu.VMEM((pairs...]
where the time goes in v1:
time: 16.6 us; the launch traced here: 16.5 us
  Pallas kernels  15.8 us (95%)
  local copies, waits for them, and re-layouts  0.66 us (4%)
    pallas_call x1, Pallas kernels, on_device(): pl.pallas_call(functools.partial(kernel, n), out_shape=pltpu.VMEM((pairs...  15.8 us
    unnamed x1, local copies, waits for them, and re-layouts  0.66 us

profile of v1, /device:TPU:0, one launch (start us, length us, event | category | flops | bytes accessed | tf_op | source)
XLA Modules:
  0.0 16.5 jit_solution(16104355898192664863)
XLA Ops:
  0.0 15.8 %shard_map.73 = bf16[512,128]{1,0:T(8,128)(2,1)S(1)} custom-call(bf16[512,128]{1,0:T(8,128)(2,1)} %bitcast.9, bf16[64,256,128]{2,1,0:T(8,128)(2,1)} %bitcast.7, bf16[64,256,128]{2,1,0:T(8,128)(2,1)} %bitcast.8, f32[2,16,32]{2,1,0:T(8,128)} %gate_ref.1, s32[16]{0:T(128)} %len_ref.1, s32[4,2,16]{2,1,0:T(2,128)} %bitcast.10, s32[4,16]{1,0:T(4,128)} %bitcast.11), custom_call_target="tpu_custom_call" | custom-call | tf_op jit(solution)/shard_map/pallas_call | solution.py:316
  15.8 0.7 %copy.9 = bf16[16,32,128]{2,1,0:T(8,128)(2,1)} copy(bf16[16,32,128]{2,1,0:T(8,128)(2,1)S(1)} %bitcast.6) | data formatting | bytes 262144

commit v2 on v1

v2 whole, which is shorter than its diff:
```python
import functools
import math

import jax
import jax.numpy as jnp
from jax import lax
from jax.experimental import pallas as pl
from jax.experimental.pallas import tpu as pltpu
from jax.sharding import PartitionSpec as P

BLOCK = 128
LANES = 128
ROWS = 8
NEG = -1e30
LOG2E = 1.0 / math.log(2.0)
MESH = pl.DeviceIdType.MESH


def owners_of(n, chunks):
    if chunks >= 2 * n and n > 2:
        return [0, 0] + [2] + [2 - c % 2 for c in range(chunks - 3)]
    return [c * n // chunks for c in range(chunks)]


def orders_of(n, owners, parts, cuts):
    first = [sum(owners[p * cuts + i] == 0 for i in range(cuts)) for p in range(parts)]
    late = sorted(range(parts), key=lambda p: first[p])
    early = sorted(range(parts), key=lambda p: -first[p])
    return [late if d in (0, n - 1) else early for d in range(n)]


def plan_of(n, pairs, group):
    size = min(pairs, LANES // group)
    parts = pairs // size
    cuts = max(2, n // parts)
    return size, parts, cuts


def kernel(
    n, q_hbm, k_hbm, v_hbm, gate_hbm, len_hbm, chosen_hbm, count_hbm, o_ref,
    q_ref, gate_ref, len_ref, chosen_ref, count_ref,
    k_buf, v_buf, msg, r_msg, gates, held_scores, held_left,
    turn_sem, in_sem, k_sem, v_sem, ms_sem, mr_sem, gs_sem, gr_sem,
):
    pairs, tokens, width = k_hbm.shape
    group = q_ref.shape[0] // pairs
    blocks = tokens // BLOCK
    heads, slots = chosen_ref.shape[:2]
    size, parts, cuts = plan_of(n, pairs, group)
    own = size // cuts
    chunks = parts * cuts
    owners = owners_of(n, chunks)
    holders = sorted(set(owners))
    rank = {c: at for at, c in enumerate(p * cuts + i for p in orders_of(n, owners, parts, cuts)[-1] for i in range(cuts))}
    owned = {o: sorted((c for c in range(chunks) if owners[c] == o), key=rank.get) for o in holders}
    most = max(len(v) for v in owned.values())
    span = own * group
    pooled_rows = -(-own * blocks // ROWS) * ROWS
    stat_at = span + pooled_rows
    half = ROWS // 2
    assert span * 2 <= LANES
    orders = orders_of(n, owners, parts, cuts)
    per_tile = ROWS // blocks
    scale = 1.0 / math.sqrt(width)
    me = lax.axis_index("seq")

    def mine(values):
        out = values[0]
        for d in range(1, n):
            if any(v != values[0] for v in values):
                out = jnp.where(me == d, values[d], out)
        return out

    part_at = [mine([orders[d][k] for d in range(n)]) for k in range(parts)]

    def load(k, hbm, buf, sem):
        return pltpu.make_async_copy(hbm.at[pl.ds(part_at[k] * size, size)], buf.at[k], sem.at[k])

    small = [
        pltpu.make_async_copy(src, dst, in_sem.at[i])
        for i, (src, dst) in enumerate([
            (q_hbm, q_ref), (len_hbm, len_ref), (chosen_hbm, chosen_ref),
            (count_hbm, count_ref), (gate_hbm, gate_ref),
        ])
    ]
    for copy in small:
        copy.start()
    queue = [(0, k_hbm, k_buf, k_sem)]
    for k in range(1, parts):
        queue += [(k, k_hbm, k_buf, k_sem), (k - 1, v_hbm, v_buf, v_sem)]
    queue.append((parts - 1, v_hbm, v_buf, v_sem))
    for item in queue:
        pl.semaphore_signal(turn_sem, 1)
        pl.semaphore_wait(turn_sem, 1)
        load(*item).start()

    barrier = pltpu.get_barrier_semaphore()
    holds = functools.reduce(jnp.logical_or, [me == o for o in holders])

    @pl.when(holds)
    def _():
        for r in range(1, n):
            pl.semaphore_signal(
                barrier, inc=1, device_id={"seq": lax.rem(me + r, n)}, device_id_type=MESH
            )

    lane = lax.broadcasted_iota(jnp.int32, (ROWS, LANES), 1)
    row = lax.broadcasted_iota(jnp.int32, (ROWS, LANES), 0)

    def gate_row(branch, first):
        pieces = []
        at = first
        while at < first + own:
            b, h = divmod(at, heads)
            run = min(heads - h, first + own - at)
            pieces.append(gate_ref[branch, b : b + 1, h * group : (h + run) * group])
            at += run
        if span < LANES:
            pieces.append(jnp.zeros((1, LANES - span), jnp.float32))
        return jax.nn.sigmoid(jnp.concatenate(pieces, axis=1))

    def chunk_of(d, at):
        return orders[d][at // cuts] * cuts + at % cuts

    goal = [mine([owners[chunk_of(d, at)] for d in range(n)]) for at in range(chunks)]
    seat = [mine([owned[owners[chunk_of(d, at)]].index(chunk_of(d, at)) for d in range(n)]) for at in range(chunks)]
    away = [mine([int(owners[chunk_of(d, at)] != d) for d in range(n)]) == 1 for at in range(chunks)]

    def send(at):
        slot = lax.rem(me - goal[at] + n, n) - 1
        return pltpu.make_async_remote_copy(
            src_ref=msg.at[at], dst_ref=r_msg.at[seat[at], slot],
            send_sem=ms_sem.at[at], recv_sem=mr_sem.at[seat[at], slot],
            device_id={"seq": goal[at]}, device_id_type=MESH,
        )

    def arrival(at, slot):
        return pltpu.make_async_remote_copy(
            src_ref=msg.at[0], dst_ref=r_msg.at[at, slot],
            send_sem=ms_sem.at[0], recv_sem=mr_sem.at[at, slot],
            device_id={"seq": lax.rem(me + 1 + slot, n)}, device_id_type=MESH,
        )

    def limit_of(k, i, j, filled):
        b, h = part_at[k] * (size // heads) + i // heads, i % heads
        block = me * blocks + j
        hits = [(chosen_ref[h, slot, b] == block) & (slot < count_ref[h, b]) for slot in range(slots)]
        return jnp.where(functools.reduce(jnp.logical_or, hits), filled, 0)

    def score(k):
        first = pl.multiple_of(part_at[k] * (size * group), size * group)
        for i in range(0, size, 2):
            rows = q_ref[pl.ds(first + i * group, 2 * group), :]
            for o in range(2):
                both = lax.dot_general(
                    rows, k_buf[k, i + o], (((1,), (1,)), ((), ())), preferred_element_type=jnp.float32
                )
                held_scores[k, i + o] = both[o * group : (o + 1) * group]

    def weigh(k):
        columns = []
        for i in range(size):
            if i % heads == 0:
                length = len_ref[part_at[k] * (size // heads) + i // heads]
                filled = [jnp.clip(length - (me * blocks + j) * BLOCK, 0, BLOCK) for j in range(blocks)]
                fills = [jnp.full((ROWS, LANES), f, jnp.int32) for f in filled]
                live = [jnp.where(lane < f, 1.0, 0.0) for f in fills]
                root = [lax.rsqrt(jnp.maximum(f, 1).astype(jnp.float32)) * scale for f in fills]
                none = [jnp.where(f > 0, 0.0, NEG) for f in fills]
            at = i % own % per_tile
            masked, stats = [], jnp.zeros((ROWS, LANES), jnp.float32)
            for j in range(blocks):
                scores = held_scores[k, i, :, j * BLOCK : (j + 1) * BLOCK]
                total = jnp.sum(scores * live[j], axis=1, keepdims=True)
                stats = jnp.where(lane == 1 + j, total * root[j] + none[j], stats)
                masked.append(jnp.where(lane < limit_of(k, i, j, filled[j]), scores, NEG))
            top = jnp.max(functools.reduce(jnp.maximum, masked), axis=1, keepdims=True)
            top = jnp.maximum(top, NEG / 10)
            weights = [jnp.exp2((m - top) * (scale * LOG2E)) for m in masked]
            weight_sum = jnp.sum(functools.reduce(jnp.add, weights), axis=1, keepdims=True)
            stats = jnp.where(lane == 0, top * scale, jnp.where(lane == 1 + blocks, weight_sum, stats))
            columns.append(stats)
            lives = [jnp.where(row == at * blocks + j, live[j], 0.0) for j in range(blocks)]
            left = jnp.concatenate([jnp.concatenate(weights, axis=1), jnp.concatenate(lives, axis=1)], axis=0)
            held_left[k, i] = left.astype(jnp.bfloat16)
        if size * group < LANES:
            columns.append(jnp.zeros((LANES - size * group, LANES), jnp.float32))
        stats = jnp.concatenate(columns, axis=0).T[:ROWS]
        high = stats.astype(jnp.bfloat16).astype(jnp.float32)
        return high, stats - high

    def gather(k, high, low):
        for cut in range(cuts):
            c = k * cuts + cut
            outs, tiles = [], []
            for i in range(cut * own, (cut + 1) * own):
                at = (i - cut * own) % per_tile
                if at == 0:
                    members = range(i, min(i + per_tile, (cut + 1) * own))
                    length_rows = jnp.zeros((ROWS, LANES), jnp.int32)
                    for m, p in enumerate(members):
                        length = len_ref[part_at[k] * (size // heads) + p // heads]
                        length_rows = jnp.where(lax.div(row, blocks) == m, length, length_rows)
                    start_rows = (me * blocks + lax.rem(row, blocks)) * BLOCK
                    filled_rows = jnp.clip(length_rows - start_rows, 0, BLOCK)
                    root_rows = lax.rsqrt(jnp.maximum(filled_rows, 1).astype(jnp.float32))
                    pooled = jnp.zeros((ROWS, width), jnp.float32)
                summed = jnp.dot(held_left[k, i], v_buf[k, i], preferred_element_type=jnp.float32)
                outs.append(summed[:group])
                pooled = pooled + summed[group:]
                if at == per_tile - 1 or i == (cut + 1) * own - 1:
                    tiles.append(pooled * root_rows)

            def turned(x, to):
                return pltpu.roll(x, (to - cut * span) % LANES, 1) if to != cut * span else x

            parted = jnp.where(lane < LANES // 2, turned(high, 0), turned(low, LANES // 2))
            msg[c] = jnp.concatenate(outs + tiles + [parted[:half]], axis=0).astype(jnp.bfloat16)

    defer = me == 0

    def meet():
        pl.semaphore_wait(barrier, jnp.where(holds, len(holders) - 1, len(holders)))

    def launch(k, when):
        for cut in range(cuts):
            c = k * cuts + cut

            @pl.when(jnp.logical_and(away[c], when))
            def _(c=c):
                send(c).start()

    for copy in small:
        copy.wait()
    load(0, k_hbm, k_buf, k_sem).wait()
    score(0)
    for c in range(chunks):
        gates[c] = jnp.where(row == 0, gate_row(1, c * own), gate_row(0, c * own))
    stats = {}
    if parts == 1:
        stats[0] = weigh(0)
    for k in range(parts):
        if k + 1 < parts:
            load(k + 1, k_hbm, k_buf, k_sem).wait()
            score(k + 1)
            if k not in stats:
                stats[k] = weigh(k)
        load(k, v_hbm, v_buf, v_sem).wait()
        gather(k, *stats[k])
        if k + 2 == parts:
            stats[k + 1] = weigh(k + 1)
        if k == 0:
            pl.when(jnp.logical_not(defer))(meet)
        launch(k, jnp.logical_not(defer))
    pl.when(defer)(meet)
    for k in range(parts):
        launch(k, defer)

    def pick(at):
        c = 0
        for o in holders:
            if at < len(owned[o]):
                c = jnp.where(me == o, owned[o][at], c)
        return c

    def has(at):
        return functools.reduce(jnp.logical_or, [me == o for o in holders if at < len(owned[o])])

    def spot(c):
        return pl.ds(pl.multiple_of(c * span, span), span)

    def deliver(rows, sem, c, to):
        return pltpu.make_async_remote_copy(
            src_ref=rows, dst_ref=rows, send_sem=sem, recv_sem=gr_sem.at[c],
            device_id={"seq": to}, device_id_type=MESH,
        )

    def share(at, i):
        to = jnp.where(i < me, i, i + 1)
        return deliver(o_ref.at[spot(pick(at))], gs_sem.at[at, i], pick(at), to)

    def finish(at):
        c = pick(at)
        here = 0
        for o in holders:
            if at < len(owned[o]):
                spots = [chunk_of(o, i) for i in range(chunks)]
                here = jnp.where(me == o, spots.index(owned[o][at]), here)
        for slot in range(n - 1):
            arrival(at, slot).wait_recv()
        halves = row[:half]
        parts_in = [r_msg.at[at, slot] for slot in range(n - 1)] + [msg.at[here]]
        all_stats = []
        for ref in parts_in:
            parted = ref[stat_at : stat_at + half, :].astype(jnp.float32)
            all_stats.append(parted + pltpu.roll(parted, LANES // 2, 1))
        top = functools.reduce(jnp.maximum, all_stats)
        block_row = (halves >= 1) & (halves <= blocks)
        block_top = jnp.max(jnp.where(block_row, top, NEG), axis=0, keepdims=True)
        top = jnp.where(halves == 0, top, block_top)
        shares = [jnp.where(halves <= blocks, jnp.exp(s - top), 0.0) for s in all_stats]
        total = functools.reduce(jnp.add, [s[:1] * x[1 + blocks : 2 + blocks] for s, x in zip(shares, all_stats)])
        blocks_in = jnp.where(block_row, functools.reduce(jnp.add, shares), 0.0)
        block_total = jnp.sum(blocks_in, axis=0, keepdims=True)
        factor = gates[c][:half] / jnp.where(halves == 0, total, block_total)
        wide = lax.broadcasted_iota(jnp.int32, (span, LANES), 1)
        tall = lax.broadcasted_iota(jnp.int32, (span, LANES), 0)
        pool_lane = lax.broadcasted_iota(jnp.int32, (pooled_rows, LANES), 1)
        pool_row = lax.broadcasted_iota(jnp.int32, (pooled_rows, LANES), 0)
        within = lax.div(pool_lane, group) == lax.div(pool_row, blocks)
        out = None
        for ref, s in zip(parts_in, shares):
            factors = s * factor
            pick_rows = jnp.where(wide == tall, factors[:1], 0.0)
            level = jnp.broadcast_to(factors[1:2], (pooled_rows, LANES))
            for j in range(1, blocks):
                level = jnp.where(lax.rem(pool_row, blocks) == j, factors[1 + j : 2 + j], level)
            level = jnp.where(within, level, 0.0)
            left = jnp.concatenate([pick_rows, level], axis=0).astype(jnp.bfloat16)[:, :span]
            term = lax.dot_general(
                left, ref[:stat_at, :], (((0,), (0,)), ((), ())), preferred_element_type=jnp.float32
            )
            out = term if out is None else out + term
        o_ref[spot(c), :] = out.astype(jnp.bfloat16)
        for i in range(n - 1):
            share(at, i).start()

    for at in range(most):

        @pl.when(has(at))
        def _(at=at):
            finish(at)

    for c in range(chunks):

        @pl.when(me != owners[c])
        def _(c=c):
            deliver(o_ref.at[c * span : (c + 1) * span], gs_sem.at[0, 0], c, owners[c]).wait_recv()

    for at in range(chunks):

        @pl.when(away[at])
        def _(at=at):
            send(at).wait_send()

    for at in range(most):

        @pl.when(has(at))
        def _(at=at):
            for i in range(n - 1):
                share(at, i).wait_send()


def on_device(n, queries, key_cache, value_cache, gate_logits, lengths, chosen, counts):
    batch_rows, head_count, context, width = key_cache.shape
    pairs = batch_rows * head_count
    group = queries.shape[1] // head_count
    blocks = context // BLOCK
    size, parts, cuts = plan_of(n, pairs, group)
    own = size // cuts
    chunks = parts * cuts
    owners = owners_of(n, chunks)
    most = max(owners.count(o) for o in owners)
    assert group == ROWS and ROWS % blocks == 0 and width == LANES
    assert 2 + blocks <= ROWS // 2 and size % cuts == 0 and pairs % size == 0 and size % head_count == 0 and size % 2 == 0
    rows = own * group + -(-own * blocks // ROWS) * ROWS + ROWS // 2
    vmem = pl.BlockSpec(memory_space=pltpu.VMEM)
    hbm = pl.BlockSpec(memory_space=pl.ANY)
    dma = pltpu.SemaphoreType.DMA
    output = pl.pallas_call(
        functools.partial(kernel, n),
        out_shape=pltpu.VMEM((pairs * group, width), jnp.bfloat16),
        in_specs=[hbm] * 7,
        out_specs=vmem,
        scratch_shapes=[
            pltpu.VMEM((pairs * group, width), jnp.bfloat16),
            pltpu.VMEM(gate_logits.shape, jnp.float32),
            pltpu.SMEM(lengths.shape, jnp.int32),
            pltpu.SMEM((head_count, chosen.shape[2], batch_rows), jnp.int32),
            pltpu.SMEM((head_count, batch_rows), jnp.int32),
            pltpu.VMEM((parts, size, context, width), jnp.bfloat16),
            pltpu.VMEM((parts, size, context, width), jnp.bfloat16),
            pltpu.VMEM((chunks, rows, width), jnp.bfloat16),
            pltpu.VMEM((most, n - 1, rows, width), jnp.bfloat16),
            pltpu.VMEM((chunks, ROWS, LANES), jnp.float32),
            pltpu.VMEM((parts, size, group, context), jnp.float32),
            pltpu.VMEM((parts, size, 2 * group, context), jnp.bfloat16),
            pltpu.SemaphoreType.REGULAR, dma((5,)), dma((parts,)), dma((parts,)), dma((chunks,)), dma((most, n - 1)), dma((most, n - 1)), dma((chunks,)),
        ],
        compiler_params=pltpu.CompilerParams(collective_id=0, has_side_effects=True),
    )(
        queries.reshape(pairs * group, width),
        key_cache.reshape(pairs, context, width),
        value_cache.reshape(pairs, context, width),
        gate_logits,
        lengths,
        chosen.transpose(1, 2, 0),
        counts.transpose(1, 0),
    )
    return output.reshape(batch_rows, head_count * group, width)


def solution(mesh):
    return jax.shard_map(
        functools.partial(on_device, mesh.shape["seq"]),
        mesh=mesh,
        in_specs=(
            P(("grp", "batch"), "head", None),
            P(("grp", "batch"), "head", "seq", None),
            P(("grp", "batch"), "head", "seq", None),
            P(None, ("grp", "batch"), "head"),
            P(("grp", "batch")),
            P(("grp", "batch"), "head", None),
            P(("grp", "batch"), "head"),
        ),
        out_specs=P(("grp", "batch"), "head", None),
        check_vma=False,
    )
```

time: 16.6 us -> 15.9 us (0.958)
  Pallas kernels: 15.8 us -> 15.1 us
    pallas_call x1, Pallas kernels: 15.8 us -> 15.1 us  [on_device(): pl.pallas_call(functools.partial(kernel, n), out_shape=pltpu.VMEM((pairs...]
where the time goes in v2:
time: 15.9 us; the launch traced here: 15.7 us
  Pallas kernels  15.1 us (95%)
  local copies, waits for them, and re-layouts  0.66 us (4%)
    pallas_call x1, Pallas kernels, on_device(): pl.pallas_call(functools.partial(kernel, n), out_shape=pltpu.VMEM((pairs...  15.1 us
    unnamed x1, local copies, waits for them, and re-layouts  0.66 us

profile of v2, /device:TPU:0, one launch (start us, length us, event | category | flops | bytes accessed | tf_op | source)
XLA Modules:
  0.0 15.7 jit_solution(8158850403306062785)
XLA Ops:
  0.0 15.1 %shard_map.73 = bf16[512,128]{1,0:T(8,128)(2,1)S(1)} custom-call(bf16[512,128]{1,0:T(8,128)(2,1)} %bitcast.9, bf16[64,256,128]{2,1,0:T(8,128)(2,1)} %bitcast.7, bf16[64,256,128]{2,1,0:T(8,128)(2,1)} %bitcast.8, f32[2,16,32]{2,1,0:T(8,128)} %gate_hbm.1, s32[16]{0:T(128)} %len_hbm.1, s32[4,2,16]{2,1,0:T(2,128)} %bitcast.10, s32[4,16]{1,0:T(4,128)} %bitcast.11), custom_call_target="tpu_custom_call" | custom-call | tf_op jit(solution)/shard_map/pallas_call | solution.py:370
  15.1 0.7 %copy.9 = bf16[16,32,128]{2,1,0:T(8,128)(2,1)} copy(bf16[16,32,128]{2,1,0:T(8,128)(2,1)S(1)} %bitcast.6) | data formatting | bytes 262144

commit v3 on v2

--- a/solution.py
+++ b/solution.py
@@ -18,21 +18,21 @@
 
 def owners_of(n, chunks):
     if chunks >= 2 * n and n > 2:
-        return [0, 0] + [2] + [2 - c % 2 for c in range(chunks - 3)]
+        return [0, 0] + [2 - c % 2 for c in range(chunks - 2)]
     return [c * n // chunks for c in range(chunks)]
 
 
 def orders_of(n, owners, parts, cuts):
-    first = [sum(owners[p * cuts + i] == 0 for i in range(cuts)) for p in range(parts)]
-    late = sorted(range(parts), key=lambda p: first[p])
-    early = sorted(range(parts), key=lambda p: -first[p])
-    return [late if d in (0, n - 1) else early for d in range(n)]
+    def held(p, d):
+        return sum(owners[p * cuts + i] == d for i in range(cuts))
+
+    return [sorted(range(parts), key=lambda p: (held(p, d), held(p, 0))) for d in range(n)]
 
 
 def plan_of(n, pairs, group):
-    size = min(pairs, LANES // group)
+    size = min(pairs, LANES // (2 * group))
     parts = pairs // size
-    cuts = max(2, n // parts)
+    cuts = max(1, n // parts)
     return size, parts, cuts
 
 
@@ -85,10 +85,11 @@
     ]
     for copy in small:
         copy.start()
-    queue = [(0, k_hbm, k_buf, k_sem)]
+    keys = [(k, k_hbm, k_buf, k_sem) for k in range(parts)]
+    values = [(k, v_hbm, v_buf, v_sem) for k in range(parts)]
+    queue = [keys[0], values[0]] + keys[1:2]
     for k in range(1, parts):
-        queue += [(k, k_hbm, k_buf, k_sem), (k - 1, v_hbm, v_buf, v_sem)]
-    queue.append((parts - 1, v_hbm, v_buf, v_sem))
+        queue += keys[k + 1 : k + 2] + [values[k]]
     for item in queue:
         pl.semaphore_signal(turn_sem, 1)
         pl.semaphore_wait(turn_sem, 1)
@@ -189,46 +190,44 @@
         high = stats.astype(jnp.bfloat16).astype(jnp.float32)
         return high, stats - high
 
-    def gather(k, high, low):
-        for cut in range(cuts):
-            c = k * cuts + cut
-            outs, tiles = [], []
-            for i in range(cut * own, (cut + 1) * own):
-                at = (i - cut * own) % per_tile
-                if at == 0:
-                    members = range(i, min(i + per_tile, (cut + 1) * own))
-                    length_rows = jnp.zeros((ROWS, LANES), jnp.int32)
-                    for m, p in enumerate(members):
-                        length = len_ref[part_at[k] * (size // heads) + p // heads]
-                        length_rows = jnp.where(lax.div(row, blocks) == m, length, length_rows)
-                    start_rows = (me * blocks + lax.rem(row, blocks)) * BLOCK
-                    filled_rows = jnp.clip(length_rows - start_rows, 0, BLOCK)
-                    root_rows = lax.rsqrt(jnp.maximum(filled_rows, 1).astype(jnp.float32))
-                    pooled = jnp.zeros((ROWS, width), jnp.float32)
-                summed = jnp.dot(held_left[k, i], v_buf[k, i], preferred_element_type=jnp.float32)
-                outs.append(summed[:group])
-                pooled = pooled + summed[group:]
-                if at == per_tile - 1 or i == (cut + 1) * own - 1:
-                    tiles.append(pooled * root_rows)
-
-            def turned(x, to):
-                return pltpu.roll(x, (to - cut * span) % LANES, 1) if to != cut * span else x
-
-            parted = jnp.where(lane < LANES // 2, turned(high, 0), turned(low, LANES // 2))
-            msg[c] = jnp.concatenate(outs + tiles + [parted[:half]], axis=0).astype(jnp.bfloat16)
+    def gather(k, cut, high, low):
+        c = k * cuts + cut
+        outs, tiles = [], []
+        for i in range(cut * own, (cut + 1) * own):
+            at = (i - cut * own) % per_tile
+            if at == 0:
+                members = range(i, min(i + per_tile, (cut + 1) * own))
+                length_rows = jnp.zeros((ROWS, LANES), jnp.int32)
+                for m, p in enumerate(members):
+                    length = len_ref[part_at[k] * (size // heads) + p // heads]
+                    length_rows = jnp.where(lax.div(row, blocks) == m, length, length_rows)
+                start_rows = (me * blocks + lax.rem(row, blocks)) * BLOCK
+                filled_rows = jnp.clip(length_rows - start_rows, 0, BLOCK)
+                root_rows = lax.rsqrt(jnp.maximum(filled_rows, 1).astype(jnp.float32))
+                pooled = jnp.zeros((ROWS, width), jnp.float32)
+            summed = jnp.dot(held_left[k, i], v_buf[k, i], preferred_element_type=jnp.float32)
+            outs.append(summed[:group])
+            pooled = pooled + summed[group:]
+            if at == per_tile - 1 or i == (cut + 1) * own - 1:
+                tiles.append(pooled * root_rows)
+
+        def turned(x, to):
+            return pltpu.roll(x, (to - cut * span) % LANES, 1) if to != cut * span else x
+
+        parted = jnp.where(lane < LANES // 2, turned(high, 0), turned(low, LANES // 2))
+        msg[c] = jnp.concatenate(outs + tiles + [parted[:half]], axis=0).astype(jnp.bfloat16)
 
     defer = me == 0
 
     def meet():
         pl.semaphore_wait(barrier, jnp.where(holds, len(holders) - 1, len(holders)))
 
-    def launch(k, when):
-        for cut in range(cuts):
-            c = k * cuts + cut
-
-            @pl.when(jnp.logical_and(away[c], when))
-            def _(c=c):
-                send(c).start()
+    def launch(k, cut, when):
+        c = k * cuts + cut
+
+        @pl.when(jnp.logical_and(away[c], when))
+        def _():
+            send(c).start()
 
     for copy in small:
         copy.wait()
@@ -237,24 +236,28 @@
     for c in range(chunks):
         gates[c] = jnp.where(row == 0, gate_row(1, c * own), gate_row(0, c * own))
     stats = {}
-    if parts == 1:
-        stats[0] = weigh(0)
+    stats[0] = weigh(0)
     for k in range(parts):
-        if k + 1 < parts:
+        if 0 < k < parts - 1:
             load(k + 1, k_hbm, k_buf, k_sem).wait()
             score(k + 1)
-            if k not in stats:
-                stats[k] = weigh(k)
+            stats[k] = weigh(k)
         load(k, v_hbm, v_buf, v_sem).wait()
-        gather(k, *stats[k])
-        if k + 2 == parts:
-            stats[k + 1] = weigh(k + 1)
         if k == 0:
             pl.when(jnp.logical_not(defer))(meet)
-        launch(k, jnp.logical_not(defer))
+        for cut in range(cuts):
+            gather(k, cut, *stats[k])
+            if cut == cuts - 1 and 0 < k == parts - 2:
+                stats[k + 1] = weigh(k + 1)
+            launch(k, cut, jnp.logical_not(defer))
+        if k == 0 and parts > 1:
+            load(1, k_hbm, k_buf, k_sem).wait()
+            score(1)
+            if parts == 2:
+                stats[1] = weigh(1)
     pl.when(defer)(meet)
-    for k in range(parts):
-        launch(k, defer)
+    for c in range(chunks):
+        launch(c // cuts, c % cuts, defer)
 
     def pick(at):
         c = 0
@@ -323,13 +326,23 @@
             out = term if out is None else out + term
         o_ref[spot(c), :] = out.astype(jnp.bfloat16)
         for i in range(n - 1):
-            share(at, i).start()
+            if i == 0:
+                share(at, i).start()
+            else:
+                pl.when(me <= i)(lambda i=i: share(at, i).start())
 
     for at in range(most):
 
         @pl.when(has(at))
         def _(at=at):
             finish(at)
+
+    for at in range(most):
+        for i in range(1, n - 1):
+
+            @pl.when(jnp.logical_and(has(at), me > i))
+            def _(at=at, i=i):
+                share(at, i).start()
 
     for c in range(chunks):
 

time: 15.9 us -> 15.7 us (0.987)
  Pallas kernels: 15.1 us -> 14.9 us
    pallas_call x1, Pallas kernels: 15.1 us -> 14.9 us  [on_device(): pl.pallas_call(functools.partial(kernel, n), out_shape=pltpu.VMEM((pairs...]
where the time goes in v3:
time: 15.7 us; the launch traced here: 15.5 us
  Pallas kernels  14.9 us (95%)
  local copies, waits for them, and re-layouts  0.66 us (4%)
    pallas_call x1, Pallas kernels, on_device(): pl.pallas_call(functools.partial(kernel, n), out_shape=pltpu.VMEM((pairs...  14.9 us
    unnamed x1, local copies, waits for them, and re-layouts  0.66 us

profile of v3, /device:TPU:0, one launch (start us, length us, event | category | flops | bytes accessed | tf_op | source)
XLA Modules:
  0.0 15.5 jit_solution(4818401290752764257)
XLA Ops:
  0.0 14.9 %shard_map.73 = bf16[512,128]{1,0:T(8,128)(2,1)S(1)} custom-call(bf16[512,128]{1,0:T(8,128)(2,1)} %bitcast.9, bf16[64,256,128]{2,1,0:T(8,128)(2,1)} %bitcast.7, bf16[64,256,128]{2,1,0:T(8,128)(2,1)} %bitcast.8, f32[2,16,32]{2,1,0:T(8,128)} %gate_hbm.1, s32[16]{0:T(128)} %len_hbm.1, s32[4,2,16]{2,1,0:T(2,128)} %bitcast.10, s32[4,16]{1,0:T(4,128)} %bitcast.11), custom_call_target="tpu_custom_call" | custom-call | tf_op jit(solution)/shard_map/pallas_call | solution.py:383
  14.9 0.7 %copy.9 = bf16[16,32,128]{2,1,0:T(8,128)(2,1)} copy(bf16[16,32,128]{2,1,0:T(8,128)(2,1)S(1)} %bitcast.6) | data formatting | bytes 262144

commit v4 on v3

--- a/solution.py
+++ b/solution.py
@@ -87,9 +87,7 @@
         copy.start()
     keys = [(k, k_hbm, k_buf, k_sem) for k in range(parts)]
     values = [(k, v_hbm, v_buf, v_sem) for k in range(parts)]
-    queue = [keys[0], values[0]] + keys[1:2]
-    for k in range(1, parts):
-        queue += keys[k + 1 : k + 2] + [values[k]]
+    queue = [x for pair in zip(keys, values) for x in pair]
     for item in queue:
         pl.semaphore_signal(turn_sem, 1)
         pl.semaphore_wait(turn_sem, 1)

time: 15.7 us -> 15.7 us (level)
  no operation moved by 1% of the time
where the time goes in v4:
time: 15.7 us; the launch traced here: 15.5 us
  Pallas kernels  14.9 us (95%)
  local copies, waits for them, and re-layouts  0.66 us (4%)
    pallas_call x1, Pallas kernels, on_device(): pl.pallas_call(functools.partial(kernel, n), out_shape=pltpu.VMEM((pairs...  14.9 us
    unnamed x1, local copies, waits for them, and re-layouts  0.66 us

profile of v4, /device:TPU:0, one launch (start us, length us, event | category | flops | bytes accessed | tf_op | source)
XLA Modules:
  0.0 15.5 jit_solution(14340259108787652152)
XLA Ops:
  0.0 14.9 %shard_map.73 = bf16[512,128]{1,0:T(8,128)(2,1)S(1)} custom-call(bf16[512,128]{1,0:T(8,128)(2,1)} %bitcast.9, bf16[64,256,128]{2,1,0:T(8,128)(2,1)} %bitcast.7, bf16[64,256,128]{2,1,0:T(8,128)(2,1)} %bitcast.8, f32[2,16,32]{2,1,0:T(8,128)} %gate_hbm.1, s32[16]{0:T(128)} %len_hbm.1, s32[4,2,16]{2,1,0:T(2,128)} %bitcast.10, s32[4,16]{1,0:T(4,128)} %bitcast.11), custom_call_target="tpu_custom_call" | custom-call | tf_op jit(solution)/shard_map/pallas_call | solution.py:381
  14.9 0.7 %copy.9 = bf16[16,32,128]{2,1,0:T(8,128)(2,1)} copy(bf16[16,32,128]{2,1,0:T(8,128)(2,1)S(1)} %bitcast.6) | data formatting | bytes 262144
